TPU v7x, 32 devices: a whole 2x2x4 slice. The times are simulated.
32 devices in a mesh: row: 16 (over z, y, x), col: 2 (over core).
Axes of the slice: x: 2, y: 2, z: 4, core: 2. Of those that a mesh axis runs over, the one named last changes fastest.
Arguments:
- top_tensor: bfloat16 [2304, 2304], P('row', 'col'), may hold values from -3 to 3
- bottom_tensor: bfloat16 [2304, 2304], P(('col', 'row')), may hold values from -3 to 3
- left_proj: bfloat16 [2304, 48], replicated, may hold values from -0.125 to 0.125
- right_proj: bfloat16 [2304, 48], replicated, may hold values from -0.125 to 0.125
Outputs:
- coarse: bfloat16 [2304, 2304], P(('col', 'row'))
All inputs are finite; a program needn't handle non-finite values.
Results may differ from a plain program's by a relative error of at most 0.0065.
Values may be sent and summed in bfloat16 or wider, within the bound.
No kernel may reach another device: no remote copies, remote signals or barrier semaphores. Data moves between devices by JAX's collectives and lax.ppermute only.
A program may use at most 128 MiB of HBM per device.

v0:
```python
import jax
import jax.numpy as jnp
from jax import lax
from jax.sharding import PartitionSpec as P


def place_rows(arrived, window, rows_here, bond_dim, row_count):
    slot_ids = jnp.arange(row_count * window, dtype=jnp.int32)
    source_dev = slot_ids // window
    target_upper = source_dev * rows_here // bond_dim + slot_ids % window
    placing = (target_upper[:, None] == jnp.arange(bond_dim, dtype=jnp.int32)[None, :]).astype(
        jnp.float32
    )
    return jnp.einsum("rsb,su->rub", arrived, placing, precision=lax.Precision.HIGHEST)


def local(top_tensor, bottom_tensor, left_proj, right_proj):
    bond_dim = right_proj.shape[1]
    rows_here = top_tensor.shape[0]
    block_len = top_tensor.shape[1] // bond_dim
    lower_rows = lax.all_gather(bottom_tensor, "row", axis=0, tiled=True)
    left_table = left_proj.reshape(bond_dim, bond_dim, bond_dim)
    upper_part = top_tensor.reshape(rows_here, block_len, bond_dim)
    weighted = jnp.einsum(
        "rml,lka->ramk", upper_part, left_table, preferred_element_type=jnp.float32
    )
    weighted = weighted.astype(jnp.bfloat16).reshape(rows_here * bond_dim, block_len * bond_dim)
    window = rows_here // bond_dim + 2
    row_count = lax.axis_size("row")
    start_row = lax.axis_index("row") * rows_here
    first_upper = start_row // bond_dim
    offset_rows = start_row - first_upper * bond_dim
    group_size = 8
    groups = bond_dim // group_size
    column_sets = lower_rows.reshape(block_len * bond_dim, groups, group_size * bond_dim).transpose(
        1, 0, 2
    )

    def one_group(columns):
        product_part = jnp.dot(weighted, columns, preferred_element_type=jnp.float32).astype(
            jnp.bfloat16
        )
        product_part = product_part.reshape(rows_here, bond_dim, group_size, bond_dim)
        padded = jnp.zeros((window * bond_dim, bond_dim, group_size, bond_dim), jnp.bfloat16)
        padded = lax.dynamic_update_slice_in_dim(padded, product_part, offset_rows, 0)
        regrid = padded.reshape(window, bond_dim, bond_dim, group_size, bond_dim).transpose(
            0, 2, 3, 1, 4
        )
        regrid = regrid.reshape(window * bond_dim * group_size, bond_dim * bond_dim)
        projected = jnp.dot(regrid, right_proj, preferred_element_type=jnp.float32)
        return projected.reshape(window, bond_dim, group_size, bond_dim)

    stacked = lax.map(one_group, column_sets)
    per_down = stacked.transpose(0, 3, 2, 1, 4).reshape(bond_dim, bond_dim, window, bond_dim)
    summed = lax.psum_scatter(per_down, "col", scatter_dimension=0, tiled=True)
    summed = summed.reshape(summed.shape[0] * bond_dim, window, bond_dim)
    arrived = lax.all_to_all(summed, "row", split_axis=0, concat_axis=1, tiled=True)
    combined = place_rows(arrived, window, rows_here, bond_dim, row_count)
    out_rows = combined.shape[0]
    return combined.reshape(out_rows, bond_dim * bond_dim).astype(jnp.bfloat16)


def solution(mesh):
    return jax.shard_map(
        local,
        mesh=mesh,
        in_specs=(P("row", "col"), P(("col", "row"), None), P(), P()),
        out_specs=P(("col", "row"), None),
        check_vma=False,
    )
```

profile of v0, /device:TPU:8, one launch (start us, length us, event | category | flops | bytes accessed | tf_op | source)
XLA Modules:
  0.0 962.5 jit_solution(11929934144060463136)
XLA Ops:
  10.8 12.6 %convert_bitcast_fusion = bf16[144,48,24,48]{0,1,2,3:T(8,128)(2,1)} fusion(bf16[48,48,48,1]{0,2,3,1:T(8,128)(2,1)S(1)} %copy.47, bf16[144,24,48,1]{0,2,1,3:T(8,128)(2,1)S(1)} %bitcast.72), kind=kOutput, calls=%fused_computation.9 | convolution fusion | flops 772374528 | bytes 16478208 | tf_op jit(solution)/shard_map/rml,lka->ramk/dot_general | solution.py:24
  23.4 122.5 %copy.36 = bf16[144,48,24,48]{3,2,1,0:T(8,128)(2,1)} copy(bf16[144,48,24,48]{0,1,2,3:T(8,128)(2,1)} %convert_bitcast_fusion) | data formatting | bytes 31850496 | tf_op jit(solution)/shard_map/convert_element_type | solution.py:27
  145.9 52.9 %reshape.74 = bf16[6912,1152]{1,0:T(8,128)(2,1)} reshape(bf16[144,48,24,48]{3,2,1,0:T(8,128)(2,1)} %copy.36) | data formatting | bytes 31850496 | tf_op jit(solution)/shard_map/reshape | solution.py:27
  198.8 8.6 copy.33
  207.5 674.2 %while.12 = (s32[]{:T(128)}, f32[6,5,48,8,48]{4,2,1,3,0:T(8,128)}, bf16[6,1152,384]{1,2,0:T(8,128)(2,1)}, bf16[6912,1152]{1,0:T(8,128)(2,1)}, s32[]{:T(128)}, /*...) while((s32[]{:T(128)}, f32[6,5,48,8,48]{4,2,1,3,0:T(8,128)}, bf16[6,1152,384]{1,2,0:T(8,128)(2,1)}, ...), condition=%wide.region_1.2_spmd, body=%wide.region_0.1_spmd.sunk | while | flops 6542622720 | bytes 147924096 | solution.py:53
  207.5 16.7 %fusion.31 = bf16[6912,384]{0,1:T(8,128)(2,1)} fusion(bf16[6912,1152]{1,0:T(8,128)(2,1)} %get-tuple-element.166, bf16[6,1152,384]{1,2,0:T(8,128)(2,1)} %get-tuple-element.165, s32[]{:T(128)} %get-tuple-element.155), kind=kOutput, calls=%fused_computation.1.clone.1 | convolution fusion | flops 6117949440 | bytes 22118912 | tf_op jit(solution)/shard_map/while/body/eval_jaxpr/dot_general | solution.py:40
  224.1 8.0 copy.68
  232.1 19.1 %reshape.85 = bf16[144,48,8,48]{3,2,1,0:T(8,128)(2,1)} reshape(bf16[6912,384]{1,0:T(8,128)(2,1)} %copy.68) | data formatting | bytes 10616832 | tf_op jit(solution)/shard_map/while/body/eval_jaxpr/reshape | solution.py:43
  256.2 7.3 constant_dynamic-update-slice_fusion.2
  263.5 16.7 %copy.69 = bf16[5,48,8,48,48]{4,3,2,1,0:T(8,128)(2,1)} copy(bf16[5,48,8,48,48]{4,2,1,3,0:T(8,128)(2,1)S(1)} %bitcast.64) | data formatting | bytes 17694720 | tf_op jit(solution)/shard_map/while/body/eval_jaxpr/transpose | solution.py:46
  280.2 32.5 %reshape.86 = bf16[5,48,8,2304]{3,2,1,0:T(8,128)(2,1)} reshape(bf16[5,48,8,48,48]{4,3,2,1,0:T(8,128)(2,1)} %copy.69) | data formatting | bytes 17694720 | tf_op jit(solution)/shard_map/reshape.50
  312.7 6.0 convolution_bitcast_fusion.2
  319.8 16.6 %fusion.31 = bf16[6912,384]{0,1:T(8,128)(2,1)} fusion(bf16[6912,1152]{1,0:T(8,128)(2,1)} %get-tuple-element.166, bf16[6,1152,384]{1,2,0:T(8,128)(2,1)} %get-tuple-element.165, s32[]{:T(128)} %get-tuple-element.155), kind=kOutput, calls=%fused_computation.1.clone.1 | convolution fusion | flops 6117949440 | bytes 22118912 | tf_op jit(solution)/shard_map/while/body/eval_jaxpr/dot_general | solution.py:40
  336.4 8.0 copy.68
  344.5 19.1 %reshape.85 = bf16[144,48,8,48]{3,2,1,0:T(8,128)(2,1)} reshape(bf16[6912,384]{1,0:T(8,128)(2,1)} %copy.68) | data formatting | bytes 10616832 | tf_op jit(solution)/shard_map/while/body/eval_jaxpr/reshape | solution.py:43
  368.6 7.3 constant_dynamic-update-slice_fusion.2
  375.9 16.7 %copy.69 = bf16[5,48,8,48,48]{4,3,2,1,0:T(8,128)(2,1)} copy(bf16[5,48,8,48,48]{4,2,1,3,0:T(8,128)(2,1)S(1)} %bitcast.64) | data formatting | bytes 17694720 | tf_op jit(solution)/shard_map/while/body/eval_jaxpr/transpose | solution.py:46
  392.5 32.5 %reshape.86 = bf16[5,48,8,2304]{3,2,1,0:T(8,128)(2,1)} reshape(bf16[5,48,8,48,48]{4,3,2,1,0:T(8,128)(2,1)} %copy.69) | data formatting | bytes 17694720 | tf_op jit(solution)/shard_map/reshape.50
  425.0 6.0 convolution_bitcast_fusion.2
  432.1 16.6 %fusion.31 = bf16[6912,384]{0,1:T(8,128)(2,1)} fusion(bf16[6912,1152]{1,0:T(8,128)(2,1)} %get-tuple-element.166, bf16[6,1152,384]{1,2,0:T(8,128)(2,1)} %get-tuple-element.165, s32[]{:T(128)} %get-tuple-element.155), kind=kOutput, calls=%fused_computation.1.clone.1 | convolution fusion | flops 6117949440 | bytes 22118912 | tf_op jit(solution)/shard_map/while/body/eval_jaxpr/dot_general | solution.py:40
  448.8 8.0 copy.68
  456.8 19.1 %reshape.85 = bf16[144,48,8,48]{3,2,1,0:T(8,128)(2,1)} reshape(bf16[6912,384]{1,0:T(8,128)(2,1)} %copy.68) | data formatting | bytes 10616832 | tf_op jit(solution)/shard_map/while/body/eval_jaxpr/reshape | solution.py:43
  480.9 7.3 constant_dynamic-update-slice_fusion.2
  488.2 16.7 %copy.69 = bf16[5,48,8,48,48]{4,3,2,1,0:T(8,128)(2,1)} copy(bf16[5,48,8,48,48]{4,2,1,3,0:T(8,128)(2,1)S(1)} %bitcast.64) | data formatting | bytes 17694720 | tf_op jit(solution)/shard_map/while/body/eval_jaxpr/transpose | solution.py:46
  504.9 32.5 %reshape.86 = bf16[5,48,8,2304]{3,2,1,0:T(8,128)(2,1)} reshape(bf16[5,48,8,48,48]{4,3,2,1,0:T(8,128)(2,1)} %copy.69) | data formatting | bytes 17694720 | tf_op jit(solution)/shard_map/reshape.50
  537.4 6.0 convolution_bitcast_fusion.2
  544.5 16.6 %fusion.31 = bf16[6912,384]{0,1:T(8,128)(2,1)} fusion(bf16[6912,1152]{1,0:T(8,128)(2,1)} %get-tuple-element.166, bf16[6,1152,384]{1,2,0:T(8,128)(2,1)} %get-tuple-element.165, s32[]{:T(128)} %get-tuple-element.155), kind=kOutput, calls=%fused_computation.1.clone.1 | convolution fusion | flops 6117949440 | bytes 22118912 | tf_op jit(solution)/shard_map/while/body/eval_jaxpr/dot_general | solution.py:40
  561.1 8.0 copy.68
  569.1 19.1 %reshape.85 = bf16[144,48,8,48]{3,2,1,0:T(8,128)(2,1)} reshape(bf16[6912,384]{1,0:T(8,128)(2,1)} %copy.68) | data formatting | bytes 10616832 | tf_op jit(solution)/shard_map/while/body/eval_jaxpr/reshape | solution.py:43
  593.2 7.3 constant_dynamic-update-slice_fusion.2
  600.5 16.7 %copy.69 = bf16[5,48,8,48,48]{4,3,2,1,0:T(8,128)(2,1)} copy(bf16[5,48,8,48,48]{4,2,1,3,0:T(8,128)(2,1)S(1)} %bitcast.64) | data formatting | bytes 17694720 | tf_op jit(solution)/shard_map/while/body/eval_jaxpr/transpose | solution.py:46
  617.2 32.5 %reshape.86 = bf16[5,48,8,2304]{3,2,1,0:T(8,128)(2,1)} reshape(bf16[5,48,8,48,48]{4,3,2,1,0:T(8,128)(2,1)} %copy.69) | data formatting | bytes 17694720 | tf_op jit(solution)/shard_map/reshape.50
  649.7 6.0 convolution_bitcast_fusion.2
  656.8 16.6 %fusion.31 = bf16[6912,384]{0,1:T(8,128)(2,1)} fusion(bf16[6912,1152]{1,0:T(8,128)(2,1)} %get-tuple-element.166, bf16[6,1152,384]{1,2,0:T(8,128)(2,1)} %get-tuple-element.165, s32[]{:T(128)} %get-tuple-element.155), kind=kOutput, calls=%fused_computation.1.clone.1 | convolution fusion | flops 6117949440 | bytes 22118912 | tf_op jit(solution)/shard_map/while/body/eval_jaxpr/dot_general | solution.py:40
  673.4 8.0 copy.68
  681.5 19.1 %reshape.85 = bf16[144,48,8,48]{3,2,1,0:T(8,128)(2,1)} reshape(bf16[6912,384]{1,0:T(8,128)(2,1)} %copy.68) | data formatting | bytes 10616832 | tf_op jit(solution)/shard_map/while/body/eval_jaxpr/reshape | solution.py:43
  705.6 7.3 constant_dynamic-update-slice_fusion.2
  712.9 16.7 %copy.69 = bf16[5,48,8,48,48]{4,3,2,1,0:T(8,128)(2,1)} copy(bf16[5,48,8,48,48]{4,2,1,3,0:T(8,128)(2,1)S(1)} %bitcast.64) | data formatting | bytes 17694720 | tf_op jit(solution)/shard_map/while/body/eval_jaxpr/transpose | solution.py:46
  729.5 32.5 %reshape.86 = bf16[5,48,8,2304]{3,2,1,0:T(8,128)(2,1)} reshape(bf16[5,48,8,48,48]{4,3,2,1,0:T(8,128)(2,1)} %copy.69) | data formatting | bytes 17694720 | tf_op jit(solution)/shard_map/reshape.50
  769.2 16.6 %fusion.31 = bf16[6912,384]{0,1:T(8,128)(2,1)} fusion(bf16[6912,1152]{1,0:T(8,128)(2,1)} %get-tuple-element.166, bf16[6,1152,384]{1,2,0:T(8,128)(2,1)} %get-tuple-element.165, s32[]{:T(128)} %get-tuple-element.155), kind=kOutput, calls=%fused_computation.1.clone.1 | convolution fusion | flops 6117949440 | bytes 22118912 | tf_op jit(solution)/shard_map/while/body/eval_jaxpr/dot_general | solution.py:40
  785.8 8.0 copy.68
  793.9 19.1 %reshape.85 = bf16[144,48,8,48]{3,2,1,0:T(8,128)(2,1)} reshape(bf16[6912,384]{1,0:T(8,128)(2,1)} %copy.68) | data formatting | bytes 10616832 | tf_op jit(solution)/shard_map/while/body/eval_jaxpr/reshape | solution.py:43
  818.0 7.3 constant_dynamic-update-slice_fusion.2
  825.3 16.7 %copy.69 = bf16[5,48,8,48,48]{4,3,2,1,0:T(8,128)(2,1)} copy(bf16[5,48,8,48,48]{4,2,1,3,0:T(8,128)(2,1)S(1)} %bitcast.64) | data formatting | bytes 17694720 | tf_op jit(solution)/shard_map/while/body/eval_jaxpr/transpose | solution.py:46
  841.9 32.5 %reshape.86 = bf16[5,48,8,2304]{3,2,1,0:T(8,128)(2,1)} reshape(bf16[5,48,8,48,48]{4,3,2,1,0:T(8,128)(2,1)} %copy.69) | data formatting | bytes 17694720 | tf_op jit(solution)/shard_map/reshape.50
  881.6 16.0 %reduce-scatter.2.cloned.1.call-done = f32[24,48,5,48]{3,1,2,0:T(8,128)} async-done(((f32[48,48,5,48]{3,1,2,0:T(8,128)}), f32[24,48,5,48]{3,1,2,0:T(8,128)}) %reduce-scatter.2.cloned.1.call-update) | async-done | bytes 1105936 | tf_op jit(solution)/shard_map/reduce_scatter | solution.py:55
  908.2 6.3 all-to-all-start
  914.6 27.0 %all-to-all-done = f32[16,1,17280]{2,1,0:T(1,128)S(1)} async-done(((f32[16,1,17280]{2,1,0:T(1,128)}), f32[16,1,17280]{2,1,0:T(1,128)S(1)}, u32[]{:S(2)}, u32[]{:S(2)}) %all-to-all-start) | async-done | bytes 1105952 | tf_op jit(solution)/shard_map/all_to_all | solution.py:57
  (47 shorter events, 77.8 us)
Async XLA Ops:
  6.5 192.3 %all-gather.2.cloned.1.call-start = ((), (), s32[]{:S(2)}) async-start(), calls=%async_computation.2 | async-start | bytes 5640192 | tf_op jit(solution)/shard_map/all_gather | solution.py:21
  7.3 890.4 %reduce-scatter.2.cloned.1.call-start = ((), (), s32[]{:S(2)}) async-start(), calls=%async_computation.3 | async-start | bytes 8847360 | tf_op jit(solution)/shard_map/reduce_scatter | solution.py:55
  198.8 8.6 copy-start.1
  251.2 5.0 copy-start
  363.6 5.0 copy-start
  475.9 5.0 copy-start
  588.2 5.0 copy-start
  700.6 5.0 copy-start
  812.9 5.0 copy-start
  908.2 33.3 %all-to-all-start = ((f32[16,1,17280]{2,1,0:T(1,128)}), f32[16,1,17280]{2,1,0:T(1,128)S(1)}, u32[]{:S(2)}, u32[]{:S(2)}) async-start(f32[16,1,17280]{2,1,0:T(1,128)} %reshape.81), calls=%async_computation.1 | async-start | bytes 2211840 | tf_op jit(solution)/shard_map/all_to_all | solution.py:57
Sparse Core Ops, SparseCore 0:
  10.1 86.2 all-gather.1
  881.8 15.8 reduce-scatter.1
where the time goes:
time: 973 us; the launch traced here: 962 us
  local copies, waits for them, and re-layouts  745 us (77%)
  matrix products  150 us (15%)
  waiting for transfers between devices  43.8 us (5%)
  between operations  13.5 us (1%)
    another operation x12, local copies, waits for them, and re-layouts  224 us
    convert_element_type x1, local copies, waits for them, and re-layouts, local(): weighted.astype(jnp.bfloat16)  123 us
    reshape x6, local copies, waits for them, and re-layouts, one_group(): product_part.reshape(rows_here, bond_dim, group_size, bond_dim)  114 us
    transpose x6, local copies, waits for them, and re-layouts, one_group(): padded.reshape(window, bond_dim, bond_dim, group_size, bond_dim)  100 us
    dot_general x6, matrix products, one_group(): jnp.dot(weighted, columns, preferred_element_type=jnp.float32)  99.9 us
    reshape x1, local copies, waits for them, and re-layouts, local(): weighted.astype(jnp.bfloat16)  52.9 us
    convert_element_type x6, local copies, waits for them, and re-layouts, one_group(): jnp.dot(weighted, columns, preferred_element_type=jnp.float32)  48.2 us
    dynamic_update_slice x6, local copies, waits for them, and re-layouts, one_group(): lax.dynamic_update_slice_in_dim(padded, product_part, offset_rows, 0)  43.7 us
  transfers between devices with their start and end apart: 3, of which 2 were waited for; matrix products, arithmetic and copies ran while one was open for 20% of the time, Pallas kernels for 0%

commit v1 on v0

--- a/solution.py
+++ b/solution.py
@@ -1,7 +1,15 @@
+import functools
+
 import jax
 import jax.numpy as jnp
 from jax import lax
+from jax.experimental import pallas as pl
+from jax.experimental.pallas import tpu as pltpu
 from jax.sharding import PartitionSpec as P
+
+LANES = 256
+ROW_TILE = 16
+TURN = 128
 
 
 def place_rows(arrived, window, rows_here, bond_dim, row_count):
@@ -14,7 +22,7 @@
     return jnp.einsum("rsb,su->rub", arrived, placing, precision=lax.Precision.HIGHEST)
 
 
-def local(top_tensor, bottom_tensor, left_proj, right_proj):
+def local_general(top_tensor, bottom_tensor, left_proj, right_proj):
     bond_dim = right_proj.shape[1]
     rows_here = top_tensor.shape[0]
     block_len = top_tensor.shape[1] // bond_dim
@@ -60,6 +68,145 @@
     return combined.reshape(out_rows, bond_dim * bond_dim).astype(jnp.bfloat16)
 
 
+def spread_diagonal(tile, copies):
+    size = tile.shape[0]
+    lane = lax.broadcasted_iota(jnp.int32, tile.shape, 1)
+    parts = [
+        jnp.where((lane >= k * size) & (lane < (k + 1) * size), tile, jnp.zeros_like(tile))
+        for k in range(copies)
+    ]
+    if LANES > copies * size:
+        parts.append(jnp.zeros((LANES - copies * size, LANES), tile.dtype))
+    return jnp.concatenate(parts, axis=0)
+
+
+def kernel_body(bond_dim, downs, packs, copies, n_lower, *refs):
+    lower_refs = refs[:n_lower]
+    upper_ref, left_ref, right_ref, out_ref = refs[n_lower : n_lower + 4]
+    turned_ref, weight_ref, product_ref, paired_ref, diag_ref = refs[n_lower + 4 :]
+
+    @pl.when(pl.program_id(0) == 0)
+    def _():
+        at = 0
+        for ref in lower_refs:
+            for first in range(0, ref.shape[0], TURN):
+                turned_ref[:, at : at + TURN] = ref[first : first + TURN, :].T
+                at += TURN
+
+        def fill(k, carry):
+            diag_ref[pl.ds(pl.multiple_of(k * LANES, LANES), LANES), :] = spread_diagonal(right_ref[k], copies)
+            return carry
+
+        lax.fori_loop(0, bond_dim, fill, 0)
+
+    def weigh(m, carry):
+        mixed = jnp.dot(
+            left_ref[...], spread_diagonal(upper_ref[0, m], copies), preferred_element_type=jnp.float32
+        ).astype(jnp.bfloat16)
+        rows = pl.ds(pl.multiple_of(m * bond_dim, bond_dim), bond_dim)
+        for g in range(packs):
+            weight_ref[g // 2, rows, (g % 2) * LANES : (g % 2 + 1) * LANES] = mixed[
+                g * bond_dim : (g + 1) * bond_dim
+            ]
+        return carry
+
+    lax.fori_loop(0, bond_dim, weigh, 0)
+
+    def multiply(pair, carry):
+        product_ref[...] = jnp.dot(
+            turned_ref[...], weight_ref[pair], preferred_element_type=jnp.float32
+        )
+        rows = pl.ds(pl.multiple_of(pair * 2 * downs, ROW_TILE), 2 * downs)
+        for k in range(bond_dim):
+            part = product_ref[k * downs : (k + 1) * downs, :]
+            both = jnp.concatenate([part[:, :LANES], part[:, LANES:]], axis=0)
+            paired_ref[rows, k * LANES : (k + 1) * LANES] = both.astype(jnp.bfloat16)
+        return carry
+
+    lax.fori_loop(0, packs // 2, multiply, 0)
+    out_ref[0] = jnp.dot(
+        paired_ref[...], diag_ref[...], preferred_element_type=jnp.float32
+    ).astype(jnp.bfloat16)
+
+
+def local_aligned(top_tensor, bottom_tensor, left_proj, right_proj):
+    bond_dim = right_proj.shape[1]
+    uppers = top_tensor.shape[0] // bond_dim
+    n_col = lax.axis_size("col")
+    downs = bond_dim // n_col
+    copies = LANES // bond_dim
+    packs = -(-bond_dim // copies)
+    packs += packs % 2
+    spare = LANES - copies * bond_dim
+
+    lower_rows = bottom_tensor.shape[0]
+    lower = bottom_tensor.reshape(lower_rows, n_col, downs, bond_dim).transpose(1, 0, 3, 2)
+    lower = lower.reshape(n_col, lower_rows, bond_dim * downs)
+    lower = lax.all_to_all(lower, "col", split_axis=0, concat_axis=0, tiled=True)
+    lowers = [lax.all_gather(lower[c], "row", axis=0, tiled=True) for c in range(n_col)]
+
+    upper = lax.all_gather(top_tensor, "col", axis=1, tiled=True)
+    upper = upper.reshape(uppers, bond_dim, bond_dim, bond_dim).transpose(0, 2, 3, 1)
+    upper = jnp.pad(jnp.tile(upper, (1, 1, 1, copies)), ((0, 0), (0, 0), (0, 0), (0, spare)))
+
+    left = left_proj.reshape(bond_dim, bond_dim, bond_dim).transpose(2, 1, 0)
+    left = jnp.pad(left, ((0, packs * copies - bond_dim), (0, 0), (0, 0)))
+    left = left.reshape(packs, copies, bond_dim, bond_dim).transpose(0, 2, 1, 3)
+    left = jnp.pad(
+        left.reshape(packs * bond_dim, copies * bond_dim), ((0, 0), (0, spare))
+    )
+
+    right = right_proj.reshape(bond_dim, bond_dim, bond_dim).transpose(1, 0, 2)
+    right = jnp.pad(jnp.tile(right, (1, 1, copies)), ((0, 0), (0, 0), (0, spare)))
+
+    inner = bond_dim * bond_dim
+    whole = lambda shape: pl.BlockSpec(
+        shape, lambda u: (0,) * len(shape), pipeline_mode=pl.Buffered(1)
+    )
+    result = pl.pallas_call(
+        functools.partial(kernel_body, bond_dim, downs, packs, copies, n_col),
+        grid=(uppers,),
+        in_specs=[whole(x.shape) for x in lowers]
+        + [
+            pl.BlockSpec((1, bond_dim, bond_dim, LANES), lambda u: (u, 0, 0, 0)),
+            whole(left.shape),
+            whole(right.shape),
+        ],
+        out_specs=pl.BlockSpec((1, packs * downs, LANES), lambda u: (u, 0, 0)),
+        out_shape=jax.ShapeDtypeStruct((uppers, packs * downs, LANES), jnp.bfloat16),
+        scratch_shapes=[
+            pltpu.VMEM((bond_dim * downs, inner), jnp.bfloat16),
+            pltpu.VMEM((packs // 2, inner, 2 * LANES), jnp.bfloat16),
+            pltpu.VMEM((bond_dim * downs, 2 * LANES), jnp.float32),
+            pltpu.VMEM((packs * downs, bond_dim * LANES), jnp.bfloat16),
+            pltpu.VMEM((bond_dim * LANES, LANES), jnp.bfloat16),
+        ],
+        compiler_params=pltpu.CompilerParams(
+            dimension_semantics=("arbitrary",), vmem_limit_bytes=58 * 1024 * 1024
+        ),
+    )(*lowers, upper, left, right)
+
+    result = result.reshape(uppers, packs, downs, LANES)[..., : copies * bond_dim]
+    result = result.reshape(uppers, packs, downs, copies, bond_dim).transpose(2, 1, 3, 0, 4)
+    result = result.reshape(downs, packs * copies, uppers * bond_dim)[:, :bond_dim]
+    result = result.reshape(downs * bond_dim, uppers * bond_dim)
+    return lax.all_to_all(result, "row", split_axis=0, concat_axis=1, tiled=True)
+
+
+def local(top_tensor, bottom_tensor, left_proj, right_proj):
+    bond_dim = right_proj.shape[1]
+    n_col = lax.axis_size("col")
+    aligned = (
+        top_tensor.shape[0] % bond_dim == 0
+        and bond_dim % n_col == 0
+        and (bond_dim // n_col) % 8 == 0
+        and bond_dim % ROW_TILE == 0
+        and bottom_tensor.shape[0] * lax.axis_size("row") % TURN == 0
+    )
+    route = local_aligned if aligned else local_general
+    return route(top_tensor, bottom_tensor, left_proj, right_proj)
+
+
 def solution(mesh):
     return jax.shard_map(
         local,

time: 973 us -> 267 us (0.27)
  local copies, waits for them, and re-layouts: 745 us -> 41.5 us
  matrix products: 150 us -> 0 us
  Pallas kernels: 0 us -> 87.4 us
  waiting for transfers between devices: 43.8 us -> 94.8 us
  blocking collectives: 0 us -> 26.3 us
    another operation x12 -> x4, local copies, waits for them, and re-layouts: 224 us -> 18.7 us  [the longest x2 11.6 us: local_aligned(): jnp.tile(upper, (1, 1, 1, copies))]
    convert_element_type x9 -> x0, local copies, waits for them, and re-layouts: 172 us -> none  [the longest x1 123 us: local(): weighted.astype(jnp.bfloat16)]
    reshape x10 -> x7, local copies, waits for them, and re-layouts: 175 us -> 9.91 us  [the longest x1 2.57 us: local_aligned(): right = right_proj.reshape(bond_dim, bond_dim, bond_dim).transpose(1, 0, 2)]
    dot_general x14 -> x0, matrix products: 150 us -> none  [the longest x6 99.9 us: one_group(): jnp.dot(weighted, columns, preferred_element_type=jnp.float32)]
    transpose x6 -> x5, local copies, waits for them, and re-layouts: 100 us -> 4.54 us  [the longest x1 2.33 us: local_aligned(): right = right_proj.reshape(bond_dim, bond_dim, bond_dim).transpose(1, 0, 2)]
    all_gather x1 -> x2, waiting for transfers between devices: 0.01 us -> 94.1 us  [local_aligned(): lax.all_gather(lower[c], 'row', axis=0, tiled=True)]
    pallas_call x0 -> x1, Pallas kernels: none -> 87.4 us  [local_aligned(): pl.pallas_call(functools.partial(kernel_body, bond_dim, downs, packs, cop...]
    dynamic_update_slice x12 -> x0, local copies, waits for them, and re-layouts: 50.7 us -> none  [the longest x6 43.7 us: one_group(): lax.dynamic_update_slice_in_dim(padded, product_part, offset_rows, 0)]
  transfers between devices with their start and end apart: 3 -> 2, of which waited for: 2 -> 2; matrix products, arithmetic and copies ran while one was open for 20% -> 13% of each run, Pallas kernels for 0% -> 0%
where the time goes in v1:
time: 267 us; the launch traced here: 264 us
  waiting for transfers between devices  94.8 us (36%)
  Pallas kernels  87.4 us (33%)
  local copies, waits for them, and re-layouts  41.5 us (16%)
  blocking collectives  26.3 us (10%)
  between operations  13.5 us (5%)
    all_gather x2, waiting for transfers between devices, local_aligned(): lax.all_gather(lower[c], 'row', axis=0, tiled=True)  94.1 us
    pallas_call x1, Pallas kernels, local_aligned(): pl.pallas_call(functools.partial(kernel_body, bond_dim, downs, packs, cop...  87.4 us
    all_to_all x1, blocking collectives, local_aligned(): lax.all_to_all(result, 'row', split_axis=0, concat_axis=1, tiled=True)  20 us
    another operation x2, local copies, waits for them, and re-layouts, local_aligned(): jnp.tile(upper, (1, 1, 1, copies))  11.6 us
    another operation x2, local copies, waits for them, and re-layouts, local_aligned(): jnp.tile(right, (1, 1, copies))  7.14 us
  transfers between devices with their start and end apart: 2, of which 2 were waited for; matrix products, arithmetic and copies ran while one was open for 13% of the time, Pallas kernels for 0%

profile of v1, /device:TPU:8, one launch (start us, length us, event | category | flops | bytes accessed | tf_op | source)
XLA Modules:
  0.0 263.5 jit_solution(10760017137478245207)
XLA Ops:
  6.5 0.0 copy-start.1
  6.5 0.0 all-gather.5.cloned.1.call-start
  6.5 1.3 copy.18
  7.9 0.2 copy.19
  8.0 0.3 copy.20
  8.3 4.0 %all_to_all.24 = bf16[2,72,1152]{2,1,0:T(8,128)(2,1)S(1)} all-to-all(bf16[2,72,1152]{2,1,0:T(8,128)(2,1)S(1)} %copy.20), channel_id=1, replica_groups=mesh['row'=16,'col'=2] {'col'}, dimensions={0} | all-to-all | bytes 663552 | tf_op jit(solution)/shard_map/all_to_all | solution.py:145
  12.3 0.8 fusion
  13.1 0.0 all-gather.5.cloned.1.call-update
  13.1 0.0 all-gather.7.cloned.1.call-start
  13.1 0.7 all-gather.7.cloned.1.call-update
  13.8 0.0 copy-done.1
  13.8 2.3 all_gather.11
  16.1 2.4 reshape.45
  18.6 0.5 copy.21
  19.0 4.6 %tile.8 = bf16[3,48,48,5,48]{2,4,3,1,0:T(8,128)(2,1)} broadcast(bf16[3,48,48,48]{2,3,1,0:T(8,128)(2,1)S(1)} %copy.21), dimensions={0,1,2,4} | broadcast | bytes 3981312 | tf_op jit(solution)/shard_map/tile | solution.py:150
  23.6 7.0 %copy.22 = bf16[3,48,48,240]{3,2,1,0:T(8,128)(2,1)S(1)} copy(bf16[3,48,48,240]{2,3,1,0:T(8,128)(2,1)} %bitcast.27) | data formatting | bytes 6635520 | tf_op jit(solution)/shard_map/tile | solution.py:150
  30.6 2.6 reshape.49
  33.2 2.3 copy.25
  35.5 3.0 %tile.20 = bf16[48,48,5,48]{1,3,2,0:T(8,128)(2,1)} broadcast(bf16[48,48,48]{1,2,0:T(8,128)(2,1)} %copy.25), dimensions={0,1,3} | broadcast | bytes 1327104 | tf_op jit(solution)/shard_map/tile | solution.py:160
  38.6 4.1 %copy.26 = bf16[48,48,240]{2,1,0:T(8,128)(2,1)} copy(bf16[48,48,240]{1,2,0:T(8,128)(2,1)} %bitcast.28) | data formatting | bytes 2211840 | tf_op jit(solution)/shard_map/tile | solution.py:160
  42.7 0.0 copy-start
  42.7 2.4 pad.16.refs_2_
  45.1 0.0 copy-done
  45.1 1.3 pad.19.refs_4_
  46.4 1.7 reshape.46
  48.1 0.1 pad.17
  48.2 0.7 copy.24
  49.0 0.5 reshape.48
  49.5 0.7 pad.18.refs_3_
  50.2 28.6 %all-gather.5.cloned.1.call-done = bf16[1,1152,1152]{2,1,0:T(8,128)(2,1)} async-done(((bf16[1,72,1152]{2,1,0:T(8,128)(2,1)}), bf16[1,1152,1152]{2,1,0:T(8,128)(2,1)}) %all-gather.5.cloned.1.call-update) | async-done | bytes 2654224 | tf_op jit(solution)/shard_map/all_gather | solution.py:146
  78.7 65.5 %all-gather.7.cloned.1.call-done = bf16[1,1152,1152]{2,1,0:T(8,128)(2,1)} async-done(((bf16[1,72,1152]{2,1,0:T(8,128)(2,1)}), bf16[1,1152,1152]{2,1,0:T(8,128)(2,1)}) %all-gather.7.cloned.1.call-update) | async-done | bytes 2654224 | tf_op jit(solution)/shard_map/all_gather | solution.py:146
  144.2 87.4 %shard_map.46 = bf16[3,240,256]{2,1,0:T(8,128)(2,1)} custom-call(bf16[1152,1152]{1,0:T(8,128)(2,1)} %bitcast.31, bf16[1152,1152]{1,0:T(8,128)(2,1)} %bitcast.32, bf16[3,48,48,256]{3,2,1,0:T(8,128)(2,1)} %pad.16.refs_2_, bf16[480,256]{1,0:T(8,128)(2,1)} %pad.18.refs_3_, bf16[48,48,256]{2,1,0:T(8,128)(2,1)} %pad.19.refs_4_), custom_call_target="tpu_custom_call" | custom-call | tf_op jit(solution)/shard_map/pallas_call | solution.py:166
  231.6 1.8 reshape.51
  233.5 0.9 copy.27
  234.4 0.6 reshape.52
  235.0 0.1 copy.28
  235.1 20.0 %all_to_all.25 = bf16[16,72,144]{2,1,0:T(8,128)(2,1)S(1)} all-to-all(bf16[16,72,144]{2,1,0:T(8,128)(2,1)S(1)} %bitcast.36), channel_id=1, replica_groups=mesh['row'=16,'col'=2] {'row'}, dimensions={0} | all-to-all | bytes 663552 | tf_op jit(solution)/shard_map/all_to_all | solution.py:193
  255.1 0.1 copy.29
  255.2 1.5 all_to_all.21
  (1 shorter events, 0.0 us)
Async XLA Ops:
  6.5 7.3 %copy-start.1 = (bf16[144,1152]{1,0:T(8,128)(2,1)S(1)}, bf16[144,1152]{1,0:T(8,128)(2,1)}, u32[]{:S(2)}) copy-start(bf16[144,1152]{1,0:T(8,128)(2,1)} %param.4) | copy-start | bytes 995332
  6.5 72.2 %all-gather.5.cloned.1.call-start = ((), (), s32[]{:S(2)}) async-start(), calls=%async_computation.2 | async-start | bytes 2820096 | tf_op jit(solution)/shard_map/all_gather | solution.py:146
  13.1 131.1 %all-gather.7.cloned.1.call-start = ((), (), s32[]{:S(2)}) async-start(), calls=%async_computation.3 | async-start | bytes 2820096 | tf_op jit(solution)/shard_map/all_gather | solution.py:146
  42.7 2.4 copy-start
Sparse Core Ops, SparseCore 0:
  13.2 65.4 all-gather.4
  81.4 62.7 all-gather.6
